TPU v7x, 32 devices: a whole 2x2x4 slice. The times are simulated.
32 devices in a mesh: lat: 2 (over y), lon: 8 (over z, core), freq: 2 (over x).
Axes of the slice: x: 2, y: 2, z: 4, core: 2. Of those that a mesh axis runs over, the one named last changes fastest.
Arguments:
- spectrum: float32 [36, 36, 8, 1024], P('freq', None, 'lat', 'lon'), may hold values from 0.05 to 1
- group_speed: float32 [36], P('freq'), may hold values from 0.15 to 0.6
- sea_mask: int32 [8, 1024], P('lat', 'lon'), may hold values 0 or 1
- wind_growth: float32 [8, 1024], P('lat', 'lon'), may hold values from 0.2 to 2
- dissipation: float32 [8, 1024], P('lat', 'lon'), may hold values from 0.1 to 1
- wind_profile: float32 [1296], replicated, may hold values from 0.02 to 0.2
- nonlinear_coef: float32 [1296], replicated, may hold values from 0.05 to 0.5
- momentum: float32 [2, 1296], replicated, may hold values from -6 to 6
- quadruplet: int32 [2, 1296], replicated, may hold values from 0 to 1295, as said below
- ocean_cell: int32 [8, 1024], P('lat', 'lon'), may hold values from 0 to 8191, as said below
Outputs:
- spectrum_out: float32 [36, 36, 8, 1024], P('freq', None, 'lat', 'lon')
- ocean_stress: float32 [8192, 2], P(('lon', 'freq'))
Inputs may be any that keep to these rules, and one draw needn't show every extreme that they name: quadruplet[0, b] names a bin 1 or 2 frequencies higher (at most the highest) and 1 to 6 directions further, cyclically; quadruplet[1, b] one 1 or 2 frequencies lower (at least the lowest) and 1 to 6 directions back. ocean_cell[i, j] = j * 8 + i2 with i2 within 1 of i.
All inputs are finite; a program needn't handle non-finite values. No bound on the sum of `sea_mask` on one device may be relied on, other than what follows from the above.
Results may differ from a plain program's by a relative error of at most 0.000094.
Values sent between devices are 32-bit elements; how exact they have to be, the bound alone decides.
A program may use at most 64 MiB of HBM per device.

v0:
```python
import jax
import jax.numpy as jnp
from jax import lax
from jax.sharding import PartitionSpec as P

time_step = 0.5


def padded(shard, sides, width, wrap):
    for axis, dim in sides:
        size, length = (lax.axis_size(axis), shard.shape[dim])
        up = [(i, (i + 1) % size) for i in range(size if wrap else size - 1)]
        down = [(j, i) for i, j in up]
        last = lax.slice_in_dim(shard, length - width, length, axis=dim)
        leading = lax.slice_in_dim(shard, 0, width, axis=dim)
        before = lax.ppermute(last, axis, up)
        after = lax.ppermute(leading, axis, down)
        shard = jnp.concatenate([before, shard, after], axis=dim)
    return shard


def source_update(
    flat_bins, partners, coef_rows, profile_rows, energy, wind_flat, dissip_flat, mask_flat
):
    third = jnp.take(flat_bins, partners[0], axis=0)
    fourth = jnp.take(flat_bins, partners[1], axis=0)
    transfer = coef_rows[:, None] * (
        flat_bins * flat_bins * (third + fourth) - 2.0 * flat_bins * third * fourth
    )
    scattered = jnp.zeros_like(transfer).at[partners[0]].add(transfer).at[partners[1]].add(transfer)
    tendency = (
        wind_flat[None, :] * profile_rows[:, None] * flat_bins
        + scattered
        - 2.0 * transfer
        - dissip_flat[None, :] * energy[None, :] * flat_bins
    )
    return mask_flat[None, :] * (flat_bins + time_step * tendency)


def local(
    spectrum,
    group_speed,
    sea_mask,
    wind_growth,
    dissipation,
    wind_profile,
    nonlinear_coef,
    momentum,
    quadruplet,
    ocean_cell,
):
    highest = lax.Precision.HIGHEST
    band_freqs, ndirs, lat_rows, lon_cols = spectrum.shape
    nbins = wind_profile.shape[0]
    mask_float = sea_mask.astype(jnp.float32)
    angles = 2.0 * jnp.pi * jnp.arange(ndirs).astype(jnp.float32) / ndirs
    speed_x = (group_speed[:, None] * jnp.cos(angles)[None, :])[:, :, None, None]
    speed_y = (group_speed[:, None] * jnp.sin(angles)[None, :])[:, :, None, None]
    lat_ext = padded(spectrum, (("lat", 2),), 1, False)
    lon_ext = padded(spectrum, (("lon", 3),), 1, True)
    moved = (
        spectrum
        - jnp.maximum(speed_x, 0.0) * (spectrum - lon_ext[..., :-2])
        - jnp.minimum(speed_x, 0.0) * (lon_ext[..., 2:] - spectrum)
        - jnp.maximum(speed_y, 0.0) * (spectrum - lat_ext[:, :, :-2, :])
        - jnp.minimum(speed_y, 0.0) * (lat_ext[:, :, 2:, :] - spectrum)
    )
    moved = moved * mask_float[None, None]
    band_index = lax.axis_index("freq")
    band_bins = band_freqs * ndirs
    weights = momentum * wind_profile[None, :]
    band_weights = lax.dynamic_slice_in_dim(weights, band_index * band_bins, band_bins, 1)
    stress = (
        jnp.dot(band_weights, moved.reshape(band_bins, -1), precision=highest)
        * wind_growth.reshape(-1)[None, :]
    )
    cell_flat = ocean_cell.reshape(-1)
    all_rows = lax.axis_size("lat") * lat_rows
    share_cells = all_rows * lon_cols // lax.axis_size("freq")
    stress_cols = stress.T
    first_cell = lax.axis_index("lon") * (lon_cols * all_rows)

    def one_block(offset):
        cell_ids = first_cell + offset + jnp.arange(share_cells, dtype=jnp.int32)
        block_match = (cell_ids[:, None] == cell_flat[None, :]).astype(jnp.float32)
        return jnp.dot(block_match, stress_cols, precision=highest)

    offsets = (
        jnp.arange(lax.axis_size("freq") * share_cells // share_cells, dtype=jnp.int32)
        * share_cells
    )
    band_part = lax.psum_scatter(
        lax.map(one_block, offsets).reshape(lax.axis_size("freq") * share_cells, 2),
        "freq",
        scatter_dimension=0,
        tiled=True,
    )
    ocean_stress = lax.psum(band_part, "lat")
    margin = min(4, band_freqs)
    extended = padded(moved, (("freq", 0),), margin, False)
    ext_freqs = band_freqs + 2 * margin
    ext_bins = ext_freqs * ndirs
    first_freq = band_index * band_freqs - margin
    local_bins = jnp.arange(ext_bins, dtype=jnp.int32)
    global_bins = jnp.clip(first_freq * ndirs + local_bins, 0, nbins - 1)
    partners = jnp.clip(
        jnp.take(quadruplet, global_bins, axis=1) - first_freq * ndirs, 0, ext_bins - 1
    )
    coef_rows = jnp.take(nonlinear_coef, global_bins)
    profile_rows = jnp.take(wind_profile, global_bins)
    band_sum = jnp.sum(moved.reshape(band_bins, -1), axis=0)
    energy = lax.psum(band_sum, "freq") / nbins
    result = source_update(
        extended.reshape(ext_bins, -1),
        partners,
        coef_rows,
        profile_rows,
        energy,
        wind_growth.reshape(-1),
        dissipation.reshape(-1),
        mask_float.reshape(-1),
    )
    spectrum_out = result[margin * ndirs : (margin + band_freqs) * ndirs].reshape(moved.shape)
    return (spectrum_out, ocean_stress)


def solution(mesh):
    return jax.shard_map(
        local,
        mesh=mesh,
        in_specs=(
            P("freq", None, "lat", "lon"),
            P("freq"),
            P("lat", "lon"),
            P("lat", "lon"),
            P("lat", "lon"),
            P(),
            P(),
            P(),
            P(),
            P("lat", "lon"),
        ),
        out_specs=(P("freq", None, "lat", "lon"), P(("lon", "freq"), None)),
        check_vma=False,
    )
```

profile of v0, /device:TPU:0, one launch (start us, length us, event | category | flops | bytes accessed | tf_op | source)
XLA Modules:
  0.0 136.1 jit_solution(9292985079610908880)
XLA Ops:
  7.2 2.4 %fusion.35 = (f32[18,36,1,128]{3,2,1,0:T(1,128)S(1)}, f32[18,36,1,128]{3,2,1,0:T(1,128)S(1)}) fusion(f32[18,36,4,128]{3,2,1,0:T(4,128)} %param.16), kind=kLoop, calls=%fused_computation.78 | loop fusion | bytes 1327104 | tf_op jit(solution)/shard_map/slice | solution.py:14
  11.8 5.7 %collective-permute-start.2 = (f32[18,36,1,128]{3,1,2,0:T(8,128)}, f32[18,36,1,128]{3,1,2,0:T(8,128)}, u32[]{:S(2)}, u32[]{:S(2)}) collective-permute-start(f32[18,36,1,128]{3,1,2,0:T(8,128)} %copy.32), channel_id=1, source_target_pairs={{0,16},{1,17},{2,18},{3,19},{4,20},{5,21},{6,22},{7,23},{8,24},{9,... | collective-permute-start | bytes 995336 | tf_op jit(solution)/shard_map/ppermute | solution.py:16
  17.4 1.8 %fusion.34 = (f32[18,36,4,1]{3,2,1,0:T(4,128)S(1)}, f32[18,36,4,1]{3,2,1,0:T(4,128)}) fusion(f32[18,36,4,128]{3,2,1,0:T(4,128)S(1)} %copy-done.3), kind=kLoop, calls=%fused_computation.77 | loop fusion | bytes 41472 | tf_op jit(solution)/shard_map/slice | solution.py:14
  19.3 1.9 %copy.31 = f32[18,36,4,1]{1,2,3,0:T(4,128)S(1)} copy(f32[18,36,4,1]{3,2,1,0:T(4,128)} %get-tuple-element.58) | data formatting | bytes 20736
  21.2 3.6 %collective-permute-start.1 = (f32[18,36,4,1]{1,2,3,0:T(4,128)S(1)}, f32[18,36,4,1]{1,2,3,0:T(4,128)S(1)}, u32[]{:S(2)}, u32[]{:S(2)}) collective-permute-start(f32[18,36,4,1]{1,2,3,0:T(4,128)S(1)} %copy.31), channel_id=1, source_target_pairs={{2,0},{4,2},{6,4},{8,6},{10,8},{12,10},{14,12},{0,14},{3,1},{5,3},... | collective-permute-start | bytes 31112 | tf_op jit(solution)/shard_map/ppermute | solution.py:17
  26.5 2.9 %gather_fusion = s32[936,2]{1,0:T(8,128)S(1)} fusion(s32[2,1296]{0,1:T(8,128)S(1)} %copy.26, s32[1024]{0:T(1024)S(1)} %pad_clamp_fusion.2), kind=kCustom, calls=%fused_computation.4 | custom fusion | bytes 18720 | tf_op jit(solution)/shard_map/jit(_take)/gather | solution.py:107
  30.7 5.9 %gather_fusion.2 = f32[936]{0:T(1024)S(1)} fusion(f32[1296]{0:T(1024)S(1)} %copy-done, s32[1024]{0:T(1024)S(1)} %pad_clamp_fusion.3), kind=kCustom, calls=%fused_computation.2.clone | custom fusion | bytes 11232 | tf_op jit(solution)/shard_map/jit(_take)/gather | solution.py:109
  36.6 5.9 %gather_fusion.1 = f32[936]{0:T(1024)S(1)} fusion(f32[1296]{0:T(1024)S(1)} %copy-done.1, s32[1024]{0:T(1024)S(1)} %pad_clamp_fusion.3), kind=kCustom, calls=%fused_computation.clone | custom fusion | bytes 11232 | tf_op jit(solution)/shard_map/jit(_take)/gather | solution.py:110
  43.8 1.7 %copy.19 = f32[18,36,4,1]{3,2,1,0:T(4,128)} copy(f32[18,36,4,1]{1,2,3,0:T(4,128)S(1)} %collective-permute-done) | data formatting | bytes 20736 | tf_op jit(solution)/shard_map/ppermute | solution.py:16
  45.5 1.7 %copy.21 = f32[18,36,4,1]{3,2,1,0:T(4,128)} copy(f32[18,36,4,1]{1,2,3,0:T(4,128)S(1)} %collective-permute-done.1) | data formatting | bytes 20736 | tf_op jit(solution)/shard_map/ppermute | solution.py:17
  47.5 1.4 %copy.23 = f32[18,36,1,128]{3,2,1,0:T(1,128)S(1)} copy(f32[18,36,1,128]{3,1,2,0:T(8,128)} %collective-permute-done.2) | data formatting | bytes 663552 | tf_op jit(solution)/shard_map/ppermute | solution.py:16
  48.9 7.3 %fusion.31 = (f32[4,128]{1,0:T(4,128)S(1)}, f32[18,36,4,128]{3,2,1,0:T(4,128)S(1)}) fusion(f32[4,128]{1,0:T(4,128)S(1)} %get-tuple-element.62, f32[18,36,4,128]{3,2,1,0:T(4,128)S(1)} %copy-done.3, f32[18,36,1,128]{3,2,1,0:T(1,128)S(1)} %copy.25, f32[18,36]{1,0:T(8,128)S(1)} %get-tuple-element.67, f32[18,36,1,128]{3,2,1,0:T(1,128)S(1)} %copy.23, ...), kind=kLoop, calls=%fused_computation.75 | loop fusion | flops 5971456 | bytes 3352960 | tf_op jit(solution)/shard_map/reduce_sum | solution.py:111
  56.3 3.4 %collective-permute-start.4 = (f32[4,36,4,128]{3,2,1,0:T(4,128)S(1)}, f32[4,36,4,128]{3,2,1,0:T(4,128)S(1)}, u32[]{:S(2)}, u32[]{:S(2)}) collective-permute-start(f32[4,36,4,128]{3,2,1,0:T(4,128)S(1)} %get-tuple-element.55), channel_id=1, source_target_pairs={{0,1},{2,3},{4,5},{6,7},{8,9},{10,11},{12,13},{14,15},{16,17},{18,... | collective-permute-start | bytes 884744 | tf_op jit(solution)/shard_map/ppermute | solution.py:16
  61.9 3.8 %while.10 = (s32[]{:T(128)}, f32[2,512,2]{1,2,0:T(2,128)S(1)}, s32[2]{0:T(128)S(1)}, s32[]{:T(128)}, s32[4,128]{1,0:T(4,128)S(1)}, /*index=5*/f32[512,2]{0,1:T(2,128)S(1)}, s32[]{:T(128)}) while((s32[]{:T(128)}, f32[2,512,2]{1,2,0:T(2,128)S(1)}, s32[2]{0:T(128)S(1)}, s32[]{:T(128)}, s32[4,128]{1,0:T(4,128)S(1)}, ...), condition=%wide.region_5.8_spmd, body=%wide.region_4.7_spmd.sunk | while | flops 6554115 | bytes 14453 | solution.py:93
  66.7 5.6 %psum.14 = f32[512]{0:T(512)S(1)} all-reduce(f32[512]{0:T(512)S(1)} %bitcast.57), channel_id=1, replica_groups=mesh['lat'=2,'lon'=8,'freq'=2] {'freq'}, use_global_device_ids=true, to_apply=%region_3.0 | all-reduce | flops 512 | bytes 4096 | tf_op jit(solution)/shard_map/psum | solution.py:112
  72.3 10.1 %reduce-scatter.4.cloned.1.call-done = f32[512,2]{1,0:T(8,128)} async-done(((f32[1024,2]{1,0:T(8,128)}), f32[512,2]{1,0:T(8,128)}) %reduce-scatter.4.cloned.1.call-update) | async-done | bytes 4112
  83.5 5.7 %psum.15 = f32[512,2]{0,1:T(2,128)} all-reduce(f32[512,2]{0,1:T(2,128)S(1)} %copy.29), channel_id=1, replica_groups=mesh['lat'=2,'lon'=8,'freq'=2] {'lat'}, use_global_device_ids=true, to_apply=%region_7.10 | all-reduce | flops 1024 | bytes 8192 | tf_op jit(solution)/shard_map/psum | solution.py:98
  90.8 4.8 %gather_fusion.3 = f32[936,512]{1,0:T(8,128)} fusion(f32[936,512]{1,0:T(8,128)S(1)} %bitcast.46, s32[1024]{0:T(1024)S(1)} %pad_clamp_fusion.1), kind=kCustom, calls=%fused_computation.1.clone | custom fusion | bytes 3837600 | tf_op jit(solution)/shard_map/jit(_take)/gather | solution.py:25
  95.7 4.8 %gather_fusion.4 = f32[936,512]{1,0:T(8,128)} fusion(f32[936,512]{1,0:T(8,128)S(1)} %bitcast.47, s32[1024]{0:T(1024)S(1)} %pad_clamp_fusion), kind=kCustom, calls=%fused_computation.3.clone | custom fusion | bytes 3837600 | tf_op jit(solution)/shard_map/jit(_take)/gather | solution.py:26
  100.5 4.7 %subtract_multiply_fusion = (f32[936,512]{1,0:T(8,128)}, f32[936,512]{1,0:T(8,128)}) fusion(f32[936,512]{1,0:T(8,128)} %gather_fusion.4, f32[936,512]{1,0:T(8,128)} %gather_fusion.3, f32[936]{0:T(1024)S(1)} %get-tuple-element.71, pred[936]{0:T(1024)(128)(4,1)S(1)} %copy-done.9, pred[936]{0:T(1024)(128)(4,1)S(1)} %copy-done.10, ...), kind=kLoop, calls=%fused_computation.15 | loop fusion | flops 5750784 | bytes 9596048 | tf_op jit(solution)/shard_map/mul | solution.py:27
  105.1 10.2 %scatter_fusion = f32[936,512]{1,0:T(8,128)} fusion(f32[936,512]{1,0:T(8,128)} %get-tuple-element.54, s32[936]{0:T(1024)S(1)} %bitcast.56, f32[936,512]{1,0:T(8,128)} %get-tuple-element.53), kind=kCustom, calls=%fused_computation.5 | custom fusion | flops 479232 | bytes 5754528 | tf_op jit(solution)/shard_map/scatter-add | solution.py:30
  115.3 10.2 %scatter_fusion.1 = f32[936,512]{1,0:T(8,128)} fusion(f32[936,512]{1,0:T(8,128)} %scatter_fusion, s32[936]{0:T(1024)S(1)} %bitcast.55, f32[936,512]{1,0:T(8,128)} %get-tuple-element.53), kind=kCustom, calls=%fused_computation.6 | custom fusion | flops 479232 | bytes 5754528 | tf_op jit(solution)/shard_map/scatter-add | solution.py:30
  125.5 2.2 %fusion.10 = f32[648,512]{1,0:T(8,128)S(1)} fusion(f32[936,512]{1,0:T(8,128)} %scatter_fusion.1, f32[936,512]{1,0:T(8,128)} %get-tuple-element.53, f32[936,512]{1,0:T(8,128)S(1)} %bitcast.48, f32[512]{0:T(512)S(1)} %copy-done.8, f32[512]{0:T(512)S(1)} %bitcast_multiply_fusion), kind=kLoop, calls=%fused_computation.24 | loop fusion | flops 2322432 | bytes 5312512 | tf_op jit(solution)/shard_map/mul | solution.py:37
  127.7 1.5 %reshape.244 = f32[18,36,4,128]{3,2,1,0:T(4,128)} reshape(f32[648,512]{1,0:T(8,128)S(1)} %fusion.10) | data formatting | bytes 2654208 | tf_op jit(solution)/shard_map/reshape | solution.py:123
  (83 shorter events, 15.1 us)
Async XLA Ops:
  7.2 23.5 %copy-start = (f32[1296]{0:T(1024)S(1)}, f32[1296]{0:T(1024)}, u32[]{:S(2)}) copy-start(f32[1296]{0:T(1024)} %param.22) | copy-start | bytes 15556
  7.2 10.3 %copy-start.3 = (f32[18,36,4,128]{3,2,1,0:T(4,128)S(1)}, f32[18,36,4,128]{3,2,1,0:T(4,128)}, u32[]{:S(2)}) copy-start(f32[18,36,4,128]{3,2,1,0:T(4,128)} %param.16) | copy-start | bytes 3981316
  7.2 75.2 %reduce-scatter.4.cloned.1.call-start = ((), (), s32[]{:S(2)}) async-start(), calls=%async_computation.1 | async-start | bytes 786432
  9.7 37.5 %collective-permute-start.3 = (f32[18,36,1,128]{3,1,2,0:T(8,128)S(1)}, f32[18,36,1,128]{3,1,2,0:T(8,128)S(1)}, u32[]{:S(2)}, u32[]{:S(2)}) collective-permute-start(f32[18,36,1,128]{3,1,2,0:T(8,128)S(1)} %copy.33), channel_id=1, source_target_pairs={{16,0},{17,1},{18,2},{19,3},{20,4},{21,5},{22,6},{23,7},{24,8},{25... | collective-permute-start | bytes 995336 | tf_op jit(solution)/shard_map/ppermute | solution.py:17
  11.8 35.8 %collective-permute-start.2 = (f32[18,36,1,128]{3,1,2,0:T(8,128)}, f32[18,36,1,128]{3,1,2,0:T(8,128)}, u32[]{:S(2)}, u32[]{:S(2)}) collective-permute-start(f32[18,36,1,128]{3,1,2,0:T(8,128)} %copy.32), channel_id=1, source_target_pairs={{0,16},{1,17},{2,18},{3,19},{4,20},{5,21},{6,22},{7,23},{8,24},{9,... | collective-permute-start | bytes 995336 | tf_op jit(solution)/shard_map/ppermute | solution.py:16
  19.3 6.9 %copy-start.5 = (s32[2,1296]{1,0:T(2,128)S(1)}, s32[2,1296]{1,0:T(2,128)}, u32[]{:S(2)}) copy-start(s32[2,1296]{1,0:T(2,128)} %param.24) | copy-start | bytes 31108
  21.2 24.3 %collective-permute-start.1 = (f32[18,36,4,1]{1,2,3,0:T(4,128)S(1)}, f32[18,36,4,1]{1,2,3,0:T(4,128)S(1)}, u32[]{:S(2)}, u32[]{:S(2)}) collective-permute-start(f32[18,36,4,1]{1,2,3,0:T(4,128)S(1)} %copy.31), channel_id=1, source_target_pairs={{2,0},{4,2},{6,4},{8,6},{10,8},{12,10},{14,12},{0,14},{3,1},{5,3},... | collective-permute-start | bytes 31112 | tf_op jit(solution)/shard_map/ppermute | solution.py:17
  26.1 17.7 %collective-permute-start = (f32[18,36,4,1]{1,2,3,0:T(4,128)}, f32[18,36,4,1]{1,2,3,0:T(4,128)S(1)}, u32[]{:S(2)}, u32[]{:S(2)}) collective-permute-start(f32[18,36,4,1]{1,2,3,0:T(4,128)} %copy.30), channel_id=1, source_target_pairs={{0,2},{2,4},{4,6},{6,8},{8,10},{10,12},{12,14},{14,0},{1,3},{3,5},... | collective-permute-start | bytes 31112 | tf_op jit(solution)/shard_map/ppermute | solution.py:16
  30.7 5.9 %copy-start.1 = (f32[1296]{0:T(1024)S(1)}, f32[1296]{0:T(1024)}, u32[]{:S(2)}) copy-start(f32[1296]{0:T(1024)} %param.21) | copy-start | bytes 15556
  36.5 6.0 %copy-start.14 = (f32[18]{0:T(128)S(1)}, f32[18]{0:T(128)}, u32[]{:S(2)}) copy-start(f32[18]{0:T(128)} %param.17) | copy-start | bytes 220
  36.5 6.0 %copy-start.12 = (s32[4,128]{1,0:T(4,128)S(1)}, s32[4,128]{1,0:T(4,128)}, u32[]{:S(2)}) copy-start(s32[4,128]{1,0:T(4,128)} %param.18) | copy-start | bytes 6148
  47.2 1.7 %copy-start.4 = (f32[18,36,4,1]{3,2,1,0:T(4,128)S(1)}, f32[18,36,4,1]{3,2,1,0:T(4,128)}, u32[]{:S(2)}) copy-start(f32[18,36,4,1]{3,2,1,0:T(4,128)} %copy.19) | copy-start | bytes 31108
  48.9 12.1 %copy-start.7 = (f32[4,128]{1,0:T(4,128)S(1)}, f32[4,128]{1,0:T(4,128)}, u32[]{:S(2)}) copy-start(f32[4,128]{1,0:T(4,128)} %param.19) | copy-start | bytes 6148
  48.9 12.1 %copy-start.11 = (f32[2,1296]{1,0:T(2,128)S(1)}, f32[2,1296]{1,0:T(2,128)}, u32[]{:S(2)}) copy-start(f32[2,1296]{1,0:T(2,128)} %param.23) | copy-start | bytes 31108
  56.2 5.6 %copy-start.6 = (f32[2,512,2]{1,2,0:T(2,128)S(1)}, f32[2,512,2]{1,2,0:T(2,128)}, u32[]{:S(2)}) copy-start(f32[2,512,2]{1,2,0:T(2,128)} %custom-call.10) | copy-start | bytes 24580
  56.2 5.6 %copy-start.15 = (s32[4,128]{1,0:T(4,128)S(1)}, s32[4,128]{1,0:T(4,128)}, u32[]{:S(2)}) copy-start(s32[4,128]{1,0:T(4,128)} %param.25) | copy-start | bytes 6148
  56.2 5.6 %copy-start.16 = (s32[2]{0:T(128)S(1)}, s32[2]{0:T(128)}, u32[]{:S(2)}) copy-start(s32[2]{0:T(128)} %iota_multiply_fusion) | copy-start | bytes 28
  56.3 32.9 %collective-permute-start.4 = (f32[4,36,4,128]{3,2,1,0:T(4,128)S(1)}, f32[4,36,4,128]{3,2,1,0:T(4,128)S(1)}, u32[]{:S(2)}, u32[]{:S(2)}) collective-permute-start(f32[4,36,4,128]{3,2,1,0:T(4,128)S(1)} %get-tuple-element.55), channel_id=1, source_target_pairs={{0,1},{2,3},{4,5},{6,7},{8,9},{10,11},{12,13},{14,15},{16,17},{18,... | collective-permute-start | bytes 884744 | tf_op jit(solution)/shard_map/ppermute | solution.py:16
  59.7 29.4 %collective-permute-start.5 = (f32[4,36,4,128]{3,2,1,0:T(4,128)S(1)}, f32[4,36,4,128]{3,2,1,0:T(4,128)S(1)}, u32[]{:S(2)}, u32[]{:S(2)}) collective-permute-start(f32[4,36,4,128]{3,2,1,0:T(4,128)S(1)} %get-tuple-element.56), channel_id=1, source_target_pairs={{1,0},{3,2},{5,4},{7,6},{9,8},{11,10},{13,12},{15,14},{17,16},{19,... | collective-permute-start | bytes 884744 | tf_op jit(solution)/shard_map/ppermute | solution.py:17
  61.9 10.4 %copy-start.13 = (f32[4,128]{1,0:T(4,128)S(1)}, f32[4,128]{1,0:T(4,128)}, u32[]{:S(2)}) copy-start(f32[4,128]{1,0:T(4,128)} %param.20) | copy-start | bytes 6148
  89.6 1.3 copy-start.2
  95.7 4.8 %copy-start.9 = (pred[936]{0:T(1024)(128)(4,1)S(1)}, pred[936]{0:T(1024)(128)(4,1)}, u32[]{:S(2)}) copy-start(pred[936]{0:T(1024)(128)(4,1)} %get-tuple-element.75) | copy-start | bytes 2812
  95.7 4.8 %copy-start.10 = (pred[936]{0:T(1024)(128)(4,1)S(1)}, pred[936]{0:T(1024)(128)(4,1)}, u32[]{:S(2)}) copy-start(pred[936]{0:T(1024)(128)(4,1)} %get-tuple-element.76) | copy-start | bytes 2812
  115.3 10.2 %copy-start.8 = (f32[512]{0:T(512)S(1)}, f32[512]{0:T(512)}, u32[]{:S(2)}) copy-start(f32[512]{0:T(512)} %get-tuple-element.61) | copy-start | bytes 6148
Sparse Core Ops, SparseCore 0:
  66.9 15.4 reduce-scatter.3
where the time goes:
time: 137 us; the launch traced here: 136 us
  local copies, waits for them, and re-layouts  44.5 us (32%)
  other arithmetic  37 us (27%)
  starting transfers between devices  15.3 us (11%)
  between operations  14.4 us (11%)
  blocking collectives  11.2 us (8%)
  waiting for transfers between devices  10.1 us (7%)
  matrix products  2.08 us (2%)
    scatter-add x2, other arithmetic, source_update(): jnp.zeros_like(transfer).at[partners[0]].add(transfer).at[partners[1]]  20.4 us
    unnamed x2, waiting for transfers between devices  10.1 us
    ppermute x3, starting transfers between devices, padded(): before = lax.ppermute(last, axis, up)  9.09 us
    unnamed x42, local copies, waits for them, and re-layouts  7.62 us
    reduce_sum x1, other arithmetic, local(): band_sum = jnp.sum(moved.reshape(band_bins, -1), axis=0)  7.27 us
    ppermute x3, starting transfers between devices, padded(): after = lax.ppermute(leading, axis, down)  6.22 us
    gather x1, local copies, waits for them, and re-layouts, local(): coef_rows = jnp.take(nonlinear_coef, global_bins)  5.85 us
    gather x1, local copies, waits for them, and re-layouts, local(): profile_rows = jnp.take(wind_profile, global_bins)  5.85 us
  transfers between devices with their start and end apart: 7, of which 1 were waited for; matrix products, arithmetic and copies ran while one was open for 24% of the time, Pallas kernels for 0%

commit v1 on v0

v1 whole, which is shorter than its diff:
```python
import functools

import jax
import jax.numpy as jnp
import numpy as np
from jax import lax
from jax.experimental import pallas as pl
from jax.experimental.pallas import tpu as pltpu
from jax.sharding import PartitionSpec as P

time_step = 0.5
MESH = pl.DeviceIdType.MESH
VMEM = pltpu.VMEM


def spread(nf):
    order = list(range(4)) + list(range(nf - 4, nf)) + list(range(4, nf - 4))
    return {f: i for i, f in enumerate(order)}


def propagate_kernel(
    sizes, speed, spectrum, table, cols, mask, wind, cells,
    moved, energy, stress,
    x, pack_up, pack_down, got_up, got_down, edge_rows, lon_pack, got_left, got_right,
    part, parts,
    load_sem, lat_send, lat_recv, lon_send, lon_recv, freq_send, freq_recv, part_send, part_recv,
):
    n_lat, n_lon, n_freq, nf, nd, rows, nbins = sizes
    half = nd // 2
    pair = 2 * nd
    margin = 4 * nd
    band = nf * nd
    places = spread(nf)
    li, lo, fi = lax.axis_index("lat"), lax.axis_index("lon"), lax.axis_index("freq")
    load = pltpu.make_async_copy(spectrum, x, load_sem)
    load.start()

    east, west = lax.rem(lo + 1, n_lon), lax.rem(lo + n_lon - 1, n_lon)
    group = []
    for s in range(1, n_lat * n_freq):
        dl, df = divmod(s, n_freq)
        group.append(
            (dl, {"lat": lax.rem(li + dl, n_lat), "freq": lax.rem(fi + df, n_freq)})
        )
    barrier = pltpu.get_barrier_semaphore()
    for peer in [{"lon": east}, {"lon": west}] + [g for _, g in group]:
        pl.semaphore_signal(barrier, inc=1, device_id=peer, device_id_type=MESH)

    total_rows = pack_up.shape[0]
    pieces = ((0, 4 * half), (4 * half, 4 * half), (8 * half, total_rows - 8 * half))

    def lat_copy(k, up):
        at, size = pieces[k]
        src, dst = (pack_up, got_up) if up else (pack_down, got_down)
        i = k if up else 3 + k
        return pltpu.make_async_remote_copy(
            src.at[pl.ds(at, size)], dst.at[pl.ds(at, size)],
            lat_send.at[i], lat_recv.at[i],
            device_id={"lat": li + 1 if up else li - 1}, device_id_type=MESH,
        )

    def freq_copy(up):
        src = band if up else margin
        dst = 0 if up else margin + band
        return pltpu.make_async_remote_copy(
            moved.at[pl.ds(src, margin)], moved.at[pl.ds(dst, margin)],
            freq_send.at[int(up)], freq_recv.at[int(up)],
            device_id={"freq": fi + 1 if up else fi - 1}, device_id_type=MESH,
        )

    def lon_copy(to_east):
        return pltpu.make_async_remote_copy(
            lon_pack, got_left if to_east else got_right,
            lon_send.at[int(to_east)], lon_recv.at[int(to_east)],
            device_id={"lon": east if to_east else west}, device_id_type=MESH,
        )

    def part_copy(s):
        return pltpu.make_async_remote_copy(
            part, parts.at[s], part_send.at[s], part_recv.at[s],
            device_id=group[s][1], device_id_type=MESH,
        )

    up_ok, down_ok = li < n_lat - 1, li > 0
    pack_up[pl.ds(total_rows - 8, 8), :] = jnp.zeros((8, 128), jnp.float32)
    pack_down[pl.ds(total_rows - 8, 8), :] = jnp.zeros((8, 128), jnp.float32)
    load.wait()
    for f in range(nf):
        at = half * places[f]
        pack_up[pl.ds(at, half), :] = x[pl.ds(nd * f * rows + rows - 1, half, stride=rows), :]
        pack_down[pl.ds(at, half), :] = x[pl.ds((nd * f + half) * rows, half, stride=rows), :]
    pl.semaphore_wait(barrier, 2 + len(group))

    @pl.when(up_ok)
    def _():
        for k in range(3):
            lat_copy(k, True).start()

    @pl.when(down_ok)
    def _():
        for k in range(3):
            lat_copy(k, False).start()

    lane = lax.broadcasted_iota(jnp.int32, (pair, 128), 1)
    row = lax.broadcasted_iota(jnp.int32, (pair, 128), 0)
    row = jnp.where(row >= nd, row - nd, row)
    low = row < half
    cosine = table[pl.ds(0, pair), :]
    forward = cosine > 0.0
    rim = lane == jnp.where(forward, 0, 127)

    def shifted(e):
        return jnp.where(forward, pltpu.roll(e, 1, 1), pltpu.roll(e, 127, 1))

    def load_row(c, r):
        return x[pl.ds(pair * rows * c + r, pair, stride=rows), :]

    def pack_step(c, acc):
        for r in range(rows):
            z = jnp.where(rim, shifted(load_row(c, r)), 0.0)
            acc = acc + pltpu.roll(z, c * rows + r, 1)
        return acc

    lon_pack[...] = lax.fori_loop(0, nf // 2, pack_step, jnp.zeros((pair, 128), jnp.float32))
    lon_copy(True).start()
    lon_copy(False).start()

    @pl.when(jnp.logical_not(down_ok))
    def _():
        got_up[...] = jnp.zeros_like(got_up)

    @pl.when(jnp.logical_not(up_ok))
    def _():
        got_down[...] = jnp.zeros_like(got_down)

    @pl.when(fi == 0)
    def _():
        moved[pl.ds(0, margin), :] = jnp.zeros((margin, rows * 128), jnp.float32)

    @pl.when(fi == n_freq - 1)
    def _():
        moved[pl.ds(margin + band, margin), :] = jnp.zeros((margin, rows * 128), jnp.float32)

    def receive(k, freqs):
        @pl.when(down_ok)
        def _():
            lat_copy(k, True).wait_recv()

        @pl.when(up_ok)
        def _():
            lat_copy(k, False).wait_recv()

        for f in freqs:
            at = half * places[f]
            edge_rows[pl.ds(nd * f, half), :] = got_up[pl.ds(at, half), :]
            edge_rows[pl.ds(nd * f + half, half), :] = got_down[pl.ds(at, half), :]

    def chunk(c, sums):
        g = jnp.where(
            lax.broadcasted_iota(jnp.int32, (pair, 128), 0) < nd, speed[2 * c], speed[2 * c + 1]
        )
        ax = g * jnp.abs(table[pl.ds(0, pair), :])
        ay = g * jnp.abs(table[pl.ds(pair, pair), :])
        halo = jnp.where(forward, got_left[...], got_right[...])
        at = pl.multiple_of(pair * c, 8)
        outer = edge_rows[pl.ds(at, pair), :]
        here = pl.multiple_of(margin + pair * c, 8)
        w0 = cols[pl.ds(here, pair), 4:5]
        w1 = cols[pl.ds(here, pair), 5:6]
        e = [load_row(c, r) for r in range(rows)]
        out = []
        for r in range(rows):
            k = c * rows + r
            nx = jnp.where(rim, pltpu.roll(halo, 128 - k, 1), shifted(e[r]))
            below = e[r - 1] if r > 0 else outer
            above = e[r + 1] if r < rows - 1 else outer
            ny = jnp.where(low, below, above)
            m = (e[r] - ax * (e[r] - nx) - ay * (e[r] - ny)) * mask[r : r + 1, :].astype(jnp.float32)
            moved[pl.ds(here, pair), r * 128 : (r + 1) * 128] = m
            for i, v in enumerate((m, m * w0, m * w1)):
                s = sums[3 * r + i]
                for j in range(pair // 8):
                    s = s + v[8 * j : 8 * j + 8]
                out.append(s)
        return tuple(out)

    sums = tuple(jnp.zeros((8, 128), jnp.float32) for _ in range(3 * rows))
    lon_copy(True).wait_recv()
    lon_copy(False).wait_recv()
    receive(0, range(4))
    sums = lax.fori_loop(0, 2, chunk, sums)

    @pl.when(fi > 0)
    def _():
        freq_copy(False).start()

    receive(1, range(nf - 4, nf))
    sums = lax.fori_loop(nf // 2 - 2, nf // 2, chunk, sums)

    @pl.when(fi < n_freq - 1)
    def _():
        freq_copy(True).start()

    receive(2, range(4, nf - 4))
    sums = lax.fori_loop(2, nf // 2 - 2, chunk, sums)

    all_rows = n_lat * rows
    part[pl.ds(0, 8), :] = jnp.zeros((8, 128), jnp.float32)
    ids = (lo * 128 + lax.broadcasted_iota(jnp.int32, (all_rows, 128), 1)) * all_rows
    ids = ids + lax.broadcasted_iota(jnp.int32, (all_rows, 128), 0)
    totals = [jnp.zeros((all_rows, 128), jnp.float32) for _ in range(2)]
    for r in range(rows):
        part[r : r + 1, :] = jnp.sum(sums[3 * r], axis=0, keepdims=True)
        hit = cells[r : r + 1, :] == ids
        for i in range(2):
            tau = wind[r : r + 1, :] * jnp.sum(sums[3 * r + 1 + i], axis=0, keepdims=True)
            totals[i] = totals[i] + jnp.where(hit, tau, 0.0)
    for i in range(2):
        part[pl.ds(8 + i * all_rows, all_rows), :] = totals[i]
    for s in range(len(group)):
        part_copy(s).start()
    for s in range(len(group)):
        part_copy(s).wait()
    en = part[pl.ds(0, 8), :]
    st = part[pl.ds(8, 2 * all_rows), :]
    for s, (dl, _) in enumerate(group):
        if dl == 0:
            en = en + parts[s, pl.ds(0, 8), :]
        st = st + parts[s, pl.ds(8, 2 * all_rows), :]
    energy[...] = en / nbins
    stress[...] = pltpu.roll(st, lax.rem(128 - fi * (128 // n_freq), 128), 1)

    lon_copy(True).wait_send()
    lon_copy(False).wait_send()

    @pl.when(up_ok)
    def _():
        for k in range(3):
            lat_copy(k, True).wait_send()

    @pl.when(down_ok)
    def _():
        for k in range(3):
            lat_copy(k, False).wait_send()

    @pl.when(fi > 0)
    def _():
        freq_copy(False).wait_send()
        freq_copy(True).wait_recv()

    @pl.when(fi < n_freq - 1)
    def _():
        freq_copy(True).wait_send()
        freq_copy(False).wait_recv()


def split(v):
    high = v.astype(jnp.bfloat16)
    return high, (v - high.astype(jnp.float32)).astype(jnp.bfloat16)


def select_dot(pick, window):
    high, low = split(window)
    return jnp.dot(pick, high, preferred_element_type=jnp.float32) + jnp.dot(
        pick, low, preferred_element_type=jnp.float32
    )


def source_kernel(nf, nd, rows, moved, cols, lines, mask, wind, dissip, energy, out, trans):
    pair = 2 * nd
    chunks = nf // 2 + 4
    lane = lax.broadcasted_iota(jnp.int32, (pair, 3 * pair), 1)
    for c in range(1, chunks - 1):
        at = pair * c
        where = (lane + (at - pair)).astype(jnp.float32)
        picks = [
            jnp.where(cols[at : at + pair, i : i + 1] == where, 1.0, 0.0).astype(jnp.bfloat16)
            for i in range(2)
        ]
        both = select_dot(jnp.concatenate(picks, axis=0), moved[at - pair : at + 2 * pair, :])
        third, fourth = both[:pair], both[pair:]
        e = moved[at : at + pair, :]
        trans[at : at + pair, :] = cols[at : at + pair, 2:3] * (
            e * e * (third + fourth) - 2.0 * e * third * fourth
        )
    own = lax.broadcasted_iota(jnp.int32, (pair, 3 * pair), 0)
    for c in range(2, chunks - 2):
        at = pair * c
        window = trans[at - pair : at + 2 * pair, :]
        own_bin = (own + at).astype(jnp.float32)
        put = sum(
            jnp.where(lines[i : i + 1, at - pair : at + 2 * pair] == own_bin, 1.0, 0.0)
            for i in range(2)
        )
        back = select_dot(put.astype(jnp.bfloat16), window) - 2.0 * trans[at : at + pair, :]
        profile = cols[at : at + pair, 3:4]
        for r in range(rows):
            here = slice(r * 128, (r + 1) * 128)
            e = moved[at : at + pair, here]
            loss = dissip[r : r + 1, :] * energy[r : r + 1, :]
            tendency = wind[r : r + 1, :] * profile * e + back[:, here] - loss * e
            out[pl.ds(rows * (at - 2 * pair) + r, pair, stride=rows), :] = mask[
                r : r + 1, :
            ].astype(jnp.float32) * (e + time_step * tendency)


def local(
    axes,
    spectrum,
    group_speed,
    sea_mask,
    wind_growth,
    dissipation,
    wind_profile,
    nonlinear_coef,
    momentum,
    quadruplet,
    ocean_cell,
):
    n_lat, n_lon, n_freq = axes
    nf, nd, rows, width = spectrum.shape
    nbins = wind_profile.shape[0]
    band, margin, pair, half = nf * nd, 4 * nd, 2 * nd, nd // 2
    ext = band + 2 * margin
    all_rows = n_lat * rows
    f32 = jnp.float32
    angles = (np.float32(2.0 * np.pi) * np.arange(nd, dtype=np.float32) / np.float32(nd)).astype(
        np.float32
    )
    table = np.concatenate([np.tile(np.cos(angles), 2), np.tile(np.sin(angles), 2)])
    table = jnp.asarray(np.broadcast_to(table.astype(np.float32)[:, None], (2 * pair, width)))

    first = lax.axis_index("freq") * band
    lines = jnp.concatenate(
        [
            (quadruplet - (first - margin)).astype(f32),
            nonlinear_coef[None],
            wind_profile[None],
            momentum * wind_profile[None],
            jnp.zeros((2, nbins), f32),
        ]
    )
    lines = lax.dynamic_slice_in_dim(jnp.pad(lines, ((0, 0), (margin, margin))), first, ext, 1)
    cols = lines.T

    packed = -(-nf * half // 8) * 8
    peers = n_lat * n_freq - 1
    small = 8 + 2 * all_rows
    vmem = pl.BlockSpec(memory_space=VMEM)
    sizes = (n_lat, n_lon, n_freq, nf, nd, rows, nbins)
    dma = pltpu.SemaphoreType.DMA
    moved, energy, stress = pl.pallas_call(
        functools.partial(propagate_kernel, sizes),
        out_shape=(
            jax.ShapeDtypeStruct((ext, rows * width), f32),
            jax.ShapeDtypeStruct((8, width), f32),
            jax.ShapeDtypeStruct((2 * all_rows, width), f32),
        ),
        in_specs=[
            pl.BlockSpec(memory_space=pltpu.SMEM),
            pl.BlockSpec(memory_space=pl.ANY),
            vmem, vmem, vmem, vmem, vmem,
        ],
        out_specs=(vmem, vmem, vmem),
        scratch_shapes=[
            VMEM((band * rows, width), f32),
            VMEM((packed, width), f32),
            VMEM((packed, width), f32),
            VMEM((packed, width), f32),
            VMEM((packed, width), f32),
            VMEM((band, width), f32),
            VMEM((pair, width), f32),
            VMEM((pair, width), f32),
            VMEM((pair, width), f32),
            VMEM((small, width), f32),
            VMEM((peers, small, width), f32),
            dma, dma((6,)), dma((6,)), dma((2,)), dma((2,)), dma((2,)), dma((2,)),
            dma((peers,)), dma((peers,)),
        ],
        compiler_params=pltpu.CompilerParams(collective_id=0, has_side_effects=True),
    )(
        group_speed,
        spectrum.reshape(band * rows, width),
        table,
        cols,
        sea_mask,
        wind_growth,
        ocean_cell,
    )
    out = pl.pallas_call(
        functools.partial(source_kernel, nf, nd, rows),
        out_shape=jax.ShapeDtypeStruct((band * rows, width), f32),
        in_specs=[vmem] * 7,
        out_specs=vmem,
        scratch_shapes=[VMEM((ext, rows * width), f32)],
    )(moved, cols, lines, sea_mask, wind_growth, dissipation, energy)
    share = width // n_freq
    ocean = stress[:, :share].reshape(2, all_rows, share).transpose(2, 1, 0)
    return out.reshape(spectrum.shape), ocean.reshape(share * all_rows, 2)


def solution(mesh):
    axes = tuple(mesh.shape[a] for a in ("lat", "lon", "freq"))
    return jax.shard_map(
        functools.partial(local, axes),
        mesh=mesh,
        in_specs=(
            P("freq", None, "lat", "lon"),
            P("freq"),
            P("lat", "lon"),
            P("lat", "lon"),
            P("lat", "lon"),
            P(),
            P(),
            P(),
            P(),
            P("lat", "lon"),
        ),
        out_specs=(P("freq", None, "lat", "lon"), P(("lon", "freq"), None)),
        check_vma=False,
    )
```

time: 137 us -> 35.2 us (0.26)
  local copies, waits for them, and re-layouts: 44.5 us -> 5.46 us
  other arithmetic: 37 us -> 1.43 us
  Pallas kernels: 0 us -> 27.1 us
  starting transfers between devices: 15.3 us -> 0 us
  between operations: 14.4 us -> 0.67 us
  blocking collectives: 11.2 us -> 0 us
  waiting for transfers between devices: 10.1 us -> 0 us
  matrix products: 2.08 us -> 0 us
    pallas_call x0 -> x2, Pallas kernels: none -> 27.1 us  [the longest x1 21.7 us: local(): pl.pallas_call(functools.partial(propagate_kernel, sizes), out_shape=(jax...]
    gather x5 -> x0, local copies, waits for them, and re-layouts: 24.2 us -> none  [the longest x1 5.85 us: local(): coef_rows = jnp.take(nonlinear_coef, global_bins)]
    scatter-add x2 -> x0, other arithmetic: 20.4 us -> none  [source_update(): jnp.zeros_like(transfer).at[partners[0]].add(transfer).at[partners[1]]]
    ppermute x6 -> x0, starting transfers between devices: 15.3 us -> none  [the longest x3 9.09 us: padded(): before = lax.ppermute(last, axis, up)]
    psum x2 -> x0, blocking collectives: 11.2 us -> none  [the longest x1 5.69 us: local(): ocean_stress = lax.psum(band_part, 'lat')]
    unnamed x2 -> x0, waiting for transfers between devices: 10.1 us -> none
    unnamed x42 -> x2, local copies, waits for them, and re-layouts: 7.62 us -> 0.01 us
    reduce_sum x1 -> x0, other arithmetic: 7.27 us -> none  [local(): band_sum = jnp.sum(moved.reshape(band_bins, -1), axis=0)]
  transfers between devices with their start and end apart: 7 -> 0, of which waited for: 1 -> 0; matrix products, arithmetic and copies ran while one was open for 24% -> 0% of each run, Pallas kernels for 0% -> 0%
where the time goes in v1:
time: 35.2 us; the launch traced here: 34.7 us
  Pallas kernels  27.1 us (77%)
  local copies, waits for them, and re-layouts  5.46 us (16%)
  other arithmetic  1.43 us (4%)
  between operations  0.67 us (2%)
    pallas_call x1, Pallas kernels, local(): pl.pallas_call(functools.partial(propagate_kernel, sizes), out_shape=(jax...  21.7 us
    pallas_call x1, Pallas kernels, local(): pl.pallas_call(functools.partial(source_kernel, nf, nd, rows), out_shape=...  5.37 us
    another operation x1, local copies, waits for them, and re-layouts  1.4 us
    transpose x2, local copies, waits for them, and re-layouts, local(): cols = lines.T  1.11 us
    mul x1, other arithmetic, local(): momentum * wind_profile[None]  0.72 us
    convert_element_type x1, other arithmetic, local(): (quadruplet - (first - margin)).astype(f32)  0.71 us

profile of v1, /device:TPU:0, one launch (start us, length us, event | category | flops | bytes accessed | tf_op | source)
XLA Modules:
  0.0 34.7 jit_solution(13710671737464482965)
XLA Ops:
  0.6 0.7 %broadcast_in_dim.10 = f32[1,1296]{1,0:T(1,128)S(1)} reshape(f32[1296]{0:T(1024)} %param.17) | data formatting | bytes 10368 | tf_op jit(solution)/shard_map/broadcast_in_dim | solution.py:337
  1.3 0.7 %broadcast_in_dim.11 = f32[1,1296]{1,0:T(1,128)S(1)} reshape(f32[1296]{0:T(1024)} %param.16) | data formatting | bytes 10368 | tf_op jit(solution)/shard_map/broadcast_in_dim | solution.py:338
  2.0 0.7 %subtract_convert_fusion = f32[2,1296]{1,0:T(2,128)S(1)} fusion(s32[2,1296]{1,0:T(2,128)} %param.19, s32[]{:T(128)S(6)} %sub.9), kind=kLoop, calls=%fused_computation.1 | loop fusion | flops 5184 | bytes 20740 | tf_op jit(solution)/shard_map/convert_element_type | solution.py:336
  2.7 0.7 %broadcast_multiply_fusion = f32[2,1296]{1,0:T(2,128)S(1)} fusion(f32[2,1296]{1,0:T(2,128)} %param.18, f32[1296]{0:T(1024)} %param.16), kind=kLoop, calls=%fused_computation.3 | loop fusion | flops 2592 | bytes 25920 | tf_op jit(solution)/shard_map/mul | solution.py:339
  3.5 0.1 concatenate.3
  3.5 0.1 fusion
  3.6 0.7 %pad_dynamic-slice_fusion.lines = f32[8,936]{1,0:T(8,128)} fusion(s32[]{:T(128)S(6)} %select_n.3, f32[8,1296]{1,0:T(8,128)S(1)} %concatenate.3), kind=kLoop, calls=%fused_computation | loop fusion | bytes 71428 | tf_op jit(solution)/shard_map/dynamic_slice | solution.py:343
  4.3 1.0 %copy.16.cols = f32[936,8]{1,0:T(8,128)} copy(f32[936,8]{0,1:T(8,128)S(1)} %fusion) | data formatting | bytes 59904 | tf_op jit(solution)/shard_map/transpose | solution.py:344
  5.3 1.4 %jit_solution_.3.table = f32[144,128]{1,0:T(8,128)} broadcast(f32[144]{0:T(256)} %constant.18.clone), dimensions={0} | broadcast | bytes 74304 | tf_op jit(solution)
  6.7 21.7 %shard_map.122 = (f32[936,512]{1,0:T(8,128)}, f32[8,128]{1,0:T(8,128)}, f32[16,128]{1,0:T(8,128)}) custom-call(f32[18]{0:T(128)} %speed.1, f32[2592,128]{1,0:T(8,128)} %bitcast.9, f32[144,128]{1,0:T(8,128)} %jit_solution_.3.table, f32[936,8]{1,0:T(8,128)} %copy.16.cols, s32[4,128]{1,0:T(4,128)} %mask.3, f32[4,128]{1,0:T(4,128)} %wind.3, s32[4,128]{1,0:T(4,128)} %cells.1), custom_call_target="tpu_custom_call" | custom-call | tf_op jit(solution)/shard_map/pallas_call | solution.py:352
  28.5 0.0 copy-start
  28.5 5.4 %shard_map.123 = f32[2592,128]{1,0:T(8,128)} custom-call(f32[936,512]{1,0:T(8,128)} %get-tuple-element.5.moved, f32[936,8]{1,0:T(8,128)} %copy.16.cols, f32[8,936]{1,0:T(8,128)} %pad_dynamic-slice_fusion.lines, s32[4,128]{1,0:T(4,128)} %mask.3, f32[4,128]{1,0:T(4,128)} %wind.3, f32[4,128]{1,0:T(4,128)} %dissip.1, f32[8,128]{1,0:T(8,128)} %get-tuple-element.6.energy), custom_call_target="tpu_custom_call" | custom-call | tf_op jit(solution)/shard_map/pallas_call | solution.py:390
  33.9 0.0 copy-done
  33.9 0.1 copy.18
  34.0 0.7 %reshape.20 = f32[512,2]{0,1:T(2,128)} reshape(f32[64,8,2]{1,0,2:T(8,128)S(1)} %bitcast.11) | data formatting | bytes 8192 | tf_op jit(solution)/shard_map/reshape | solution.py:399
  (2 shorter events, 0.0 us)
Async XLA Ops:
  28.5 5.4 %copy-start = (f32[16,128]{1,0:T(8,128)S(1)}, f32[16,128]{1,0:T(8,128)}, u32[]{:S(2)}) copy-start(f32[16,128]{1,0:T(8,128)} %get-tuple-element.7) | copy-start | bytes 24580

commit v2 on v1

--- a/solution.py
+++ b/solution.py
@@ -19,11 +19,11 @@
 
 
 def propagate_kernel(
-    sizes, speed, spectrum, table, cols, mask, wind, cells,
-    moved, energy, stress,
-    x, pack_up, pack_down, got_up, got_down, edge_rows, lon_pack, got_left, got_right,
+    sizes, speed, spectrum, waves, profile, coef, momentum, quad, mask, wind, dissip, cells,
+    out, stress,
+    x, moved, trans, result, table, cols, lines, pack_up, pack_down, got_up, got_down, edge_rows, lon_pack, got_left, got_right,
     part, parts,
-    load_sem, lat_send, lat_recv, lon_send, lon_recv, freq_send, freq_recv, part_send, part_recv,
+    load_sem, store_sem, lat_send, lat_recv, lon_send, lon_recv, freq_send, freq_recv, part_send, part_recv,
 ):
     n_lat, n_lon, n_freq, nf, nd, rows, nbins = sizes
     half = nd // 2
@@ -50,7 +50,10 @@
     pieces = ((0, 4 * half), (4 * half, 4 * half), (8 * half, total_rows - 8 * half))
 
     def lat_copy(k, up):
-        at, size = pieces[k]
+        if isinstance(k, int):
+            at, size = pieces[k]
+        else:
+            at, size = pl.multiple_of(k * (4 * half), 8), 4 * half
         src, dst = (pack_up, got_up) if up else (pack_down, got_down)
         i = k if up else 3 + k
         return pltpu.make_async_remote_copy(
@@ -82,6 +85,23 @@
         )
 
     up_ok, down_ok = li < n_lat - 1, li > 0
+    near = lax.div(n_freq - fi, n_freq)
+    order = (near, 1 - near, 2)
+
+    span = lines.shape[1]
+    lines[...] = jnp.zeros_like(lines)
+    lines[0:2, 0:nbins] = (quad[...] - (fi * band - margin)).astype(jnp.float32)
+    lines[2:3, 0:nbins] = coef[...].reshape(1, nbins)
+    weight = profile[...].reshape(1, nbins)
+    lines[3:4, 0:nbins] = weight
+    lines[4:6, 0:nbins] = momentum[...] * weight
+    lines[...] = pltpu.roll(lines[...], lax.rem(margin - fi * band + span, span), 1)
+    for k in range(cols.shape[0] // 128):
+        cols[pl.ds(128 * k, 128), :] = lines[:, 128 * k : 128 * k + 128].T
+    turned = waves[...].T
+    table[pl.ds(0, pair), :] = jnp.broadcast_to(turned[0:pair, 0:1], (pair, 128))
+    table[pl.ds(pair, pair), :] = jnp.broadcast_to(turned[0:pair, 1:2], (pair, 128))
+
     pack_up[pl.ds(total_rows - 8, 8), :] = jnp.zeros((8, 128), jnp.float32)
     pack_down[pl.ds(total_rows - 8, 8), :] = jnp.zeros((8, 128), jnp.float32)
     load.wait()
@@ -89,24 +109,12 @@
         at = half * places[f]
         pack_up[pl.ds(at, half), :] = x[pl.ds(nd * f * rows + rows - 1, half, stride=rows), :]
         pack_down[pl.ds(at, half), :] = x[pl.ds((nd * f + half) * rows, half, stride=rows), :]
-    pl.semaphore_wait(barrier, 2 + len(group))
-
-    @pl.when(up_ok)
-    def _():
-        for k in range(3):
-            lat_copy(k, True).start()
-
-    @pl.when(down_ok)
-    def _():
-        for k in range(3):
-            lat_copy(k, False).start()
 
     lane = lax.broadcasted_iota(jnp.int32, (pair, 128), 1)
     row = lax.broadcasted_iota(jnp.int32, (pair, 128), 0)
     row = jnp.where(row >= nd, row - nd, row)
     low = row < half
-    cosine = table[pl.ds(0, pair), :]
-    forward = cosine > 0.0
+    forward = table[pl.ds(0, pair), :] > 0.0
     rim = lane == jnp.where(forward, 0, 127)
 
     def shifted(e):
@@ -122,6 +130,18 @@
         return acc
 
     lon_pack[...] = lax.fori_loop(0, nf // 2, pack_step, jnp.zeros((pair, 128), jnp.float32))
+    pl.semaphore_wait(barrier, 2 + len(group))
+
+    @pl.when(up_ok)
+    def _():
+        for k in order:
+            lat_copy(k, True).start()
+
+    @pl.when(down_ok)
+    def _():
+        for k in order:
+            lat_copy(k, False).start()
+
     lon_copy(True).start()
     lon_copy(False).start()
 
@@ -141,7 +161,7 @@
     def _():
         moved[pl.ds(margin + band, margin), :] = jnp.zeros((margin, rows * 128), jnp.float32)
 
-    def receive(k, freqs):
+    def receive(k, first, count):
         @pl.when(down_ok)
         def _():
             lat_copy(k, True).wait_recv()
@@ -150,8 +170,9 @@
         def _():
             lat_copy(k, False).wait_recv()
 
-        for f in freqs:
-            at = half * places[f]
+        base = pieces[2][0] if isinstance(k, int) else pl.multiple_of(k * (4 * half), 8)
+        for j in range(count):
+            f, at = first + j, base + half * j
             edge_rows[pl.ds(nd * f, half), :] = got_up[pl.ds(at, half), :]
             edge_rows[pl.ds(nd * f + half, half), :] = got_down[pl.ds(at, half), :]
 
@@ -187,21 +208,19 @@
     sums = tuple(jnp.zeros((8, 128), jnp.float32) for _ in range(3 * rows))
     lon_copy(True).wait_recv()
     lon_copy(False).wait_recv()
-    receive(0, range(4))
-    sums = lax.fori_loop(0, 2, chunk, sums)
-
-    @pl.when(fi > 0)
-    def _():
-        freq_copy(False).start()
-
-    receive(1, range(nf - 4, nf))
-    sums = lax.fori_loop(nf // 2 - 2, nf // 2, chunk, sums)
-
-    @pl.when(fi < n_freq - 1)
-    def _():
-        freq_copy(True).start()
-
-    receive(2, range(4, nf - 4))
+    for k in (near, 1 - near):
+        receive(k, k * (nf - 4), 4)
+        sums = lax.fori_loop(k * (nf // 2 - 2), k * (nf // 2 - 2) + 2, chunk, sums)
+
+        @pl.when(jnp.logical_and(k == 0, fi > 0))
+        def _():
+            freq_copy(False).start()
+
+        @pl.when(jnp.logical_and(k == 1, fi < n_freq - 1))
+        def _():
+            freq_copy(True).start()
+
+    receive(2, 4, nf - 8)
     sums = lax.fori_loop(2, nf // 2 - 2, chunk, sums)
 
     all_rows = n_lat * rows
@@ -219,6 +238,59 @@
         part[pl.ds(8 + i * all_rows, all_rows), :] = totals[i]
     for s in range(len(group)):
         part_copy(s).start()
+
+    chunks = nf // 2 + 4
+    is_low, is_high = fi == 0, fi == n_freq - 1
+    t_from = jnp.where(is_low, 1, 3)
+    t_to = jnp.where(is_high, chunks - 1, chunks - 3)
+    o_from = jnp.where(is_low, 2, 4)
+    o_to = jnp.where(is_high, chunks - 2, chunks - 4)
+    lane3 = lax.broadcasted_iota(jnp.int32, (pair, 3 * pair), 1)
+    row3 = lax.broadcasted_iota(jnp.int32, (pair, 3 * pair), 0)
+
+    def interact(c, carry):
+        at = pl.multiple_of(pair * c, 8)
+        prior = pl.multiple_of(pair * c - pair, 8)
+        where = (lane3 + prior).astype(jnp.float32)
+        picks = [
+            jnp.where(cols[pl.ds(at, pair), i : i + 1] == where, 1.0, 0.0).astype(jnp.bfloat16)
+            for i in range(2)
+        ]
+        both = select_dot(jnp.concatenate(picks, axis=0), moved[pl.ds(prior, 3 * pair), :])
+        third, fourth = both[:pair], both[pair:]
+        e = moved[pl.ds(at, pair), :]
+        trans[pl.ds(at, pair), :] = cols[pl.ds(at, pair), 2:3] * (
+            e * e * (third + fourth) - 2.0 * e * third * fourth
+        )
+        return carry
+
+    def store_copy(c):
+        here = pl.ds(pl.multiple_of(rows * pair * (c - 2), 8), rows * pair)
+        return pltpu.make_async_copy(result.at[here], out.at[here], store_sem.at[c - 2])
+
+    def finish(c, carry):
+        at = pl.multiple_of(pair * c, 8)
+        prior = pl.multiple_of(pair * c - pair, 8)
+        own_bin = (row3 + at).astype(jnp.float32)
+        line = pltpu.roll(lines[...], span - prior, 1)
+        put = jnp.where(line[0:1, : 3 * pair] == own_bin, 1.0, 0.0) + jnp.where(
+            line[1:2, : 3 * pair] == own_bin, 1.0, 0.0
+        )
+        back = select_dot(put.astype(jnp.bfloat16), trans[pl.ds(prior, 3 * pair), :])
+        back = back - 2.0 * trans[pl.ds(at, pair), :]
+        shape = cols[pl.ds(at, pair), 3:4]
+        for r in range(rows):
+            here = slice(r * 128, (r + 1) * 128)
+            e = moved[pl.ds(at, pair), here]
+            loss = dissip[r : r + 1, :] * total_energy[r : r + 1, :]
+            tendency = wind[r : r + 1, :] * shape * e + back[:, here] - loss * e
+            result[pl.ds(rows * pair * (c - 2) + r, pair, stride=rows), :] = mask[
+                r : r + 1, :
+            ].astype(jnp.float32) * (e + time_step * tendency)
+        store_copy(c).start()
+        return carry
+
+    lax.fori_loop(t_from, t_to, interact, 0)
     for s in range(len(group)):
         part_copy(s).wait()
     en = part[pl.ds(0, 8), :]
@@ -227,8 +299,34 @@
         if dl == 0:
             en = en + parts[s, pl.ds(0, 8), :]
         st = st + parts[s, pl.ds(8, 2 * all_rows), :]
-    energy[...] = en / nbins
-    stress[...] = pltpu.roll(st, lax.rem(128 - fi * (128 // n_freq), 128), 1)
+    total_energy = en / nbins
+    share = (128 // n_freq) * all_rows
+    cell = lax.broadcasted_iota(jnp.int32, (128, share), 1)
+    first_cell = (lax.broadcasted_iota(jnp.int32, (128, share), 0) - fi * (128 // n_freq)) * all_rows
+    inside = jnp.logical_and(cell >= first_cell, cell < first_cell + all_rows)
+    wide = jnp.dot(
+        st, jnp.where(inside, 1.0, 0.0),
+        precision=lax.Precision.HIGHEST, preferred_element_type=jnp.float32,
+    )
+    place = lax.broadcasted_iota(jnp.int32, (all_rows, share), 1) & (all_rows - 1)
+    own_row = place == lax.broadcasted_iota(jnp.int32, (all_rows, share), 0)
+    for i in range(2):
+        picked = jnp.where(own_row, wide[i * all_rows : (i + 1) * all_rows], 0.0)
+        stress[i : i + 1, :] = jnp.sum(picked, axis=0, keepdims=True)
+    lax.fori_loop(o_from, o_to, finish, 0)
+
+    @pl.when(fi > 0)
+    def _():
+        freq_copy(True).wait_recv()
+
+    @pl.when(fi < n_freq - 1)
+    def _():
+        freq_copy(False).wait_recv()
+
+    lax.fori_loop(1, t_from, interact, 0)
+    lax.fori_loop(t_to, chunks - 1, interact, 0)
+    lax.fori_loop(2, o_from, finish, 0)
+    lax.fori_loop(o_to, chunks - 2, finish, 0)
 
     lon_copy(True).wait_send()
     lon_copy(False).wait_send()
@@ -246,12 +344,13 @@
     @pl.when(fi > 0)
     def _():
         freq_copy(False).wait_send()
-        freq_copy(True).wait_recv()
 
     @pl.when(fi < n_freq - 1)
     def _():
         freq_copy(True).wait_send()
-        freq_copy(False).wait_recv()
+
+    for c in range(2, chunks - 2):
+        store_copy(c).wait()
 
 
 def split(v):
@@ -264,44 +363,6 @@
     return jnp.dot(pick, high, preferred_element_type=jnp.float32) + jnp.dot(
         pick, low, preferred_element_type=jnp.float32
     )
-
-
-def source_kernel(nf, nd, rows, moved, cols, lines, mask, wind, dissip, energy, out, trans):
-    pair = 2 * nd
-    chunks = nf // 2 + 4
-    lane = lax.broadcasted_iota(jnp.int32, (pair, 3 * pair), 1)
-    for c in range(1, chunks - 1):
-        at = pair * c
-        where = (lane + (at - pair)).astype(jnp.float32)
-        picks = [
-            jnp.where(cols[at : at + pair, i : i + 1] == where, 1.0, 0.0).astype(jnp.bfloat16)
-            for i in range(2)
-        ]
-        both = select_dot(jnp.concatenate(picks, axis=0), moved[at - pair : at + 2 * pair, :])
-        third, fourth = both[:pair], both[pair:]
-        e = moved[at : at + pair, :]
-        trans[at : at + pair, :] = cols[at : at + pair, 2:3] * (
-            e * e * (third + fourth) - 2.0 * e * third * fourth
-        )
-    own = lax.broadcasted_iota(jnp.int32, (pair, 3 * pair), 0)
-    for c in range(2, chunks - 2):
-        at = pair * c
-        window = trans[at - pair : at + 2 * pair, :]
-        own_bin = (own + at).astype(jnp.float32)
-        put = sum(
-            jnp.where(lines[i : i + 1, at - pair : at + 2 * pair] == own_bin, 1.0, 0.0)
-            for i in range(2)
-        )
-        back = select_dot(put.astype(jnp.bfloat16), window) - 2.0 * trans[at : at + pair, :]
-        profile = cols[at : at + pair, 3:4]
-        for r in range(rows):
-            here = slice(r * 128, (r + 1) * 128)
-            e = moved[at : at + pair, here]
-            loss = dissip[r : r + 1, :] * energy[r : r + 1, :]
-            tendency = wind[r : r + 1, :] * profile * e + back[:, here] - loss * e
-            out[pl.ds(rows * (at - 2 * pair) + r, pair, stride=rows), :] = mask[
-                r : r + 1, :
-            ].astype(jnp.float32) * (e + time_step * tendency)
 
 
 def local(
@@ -327,43 +388,37 @@
     angles = (np.float32(2.0 * np.pi) * np.arange(nd, dtype=np.float32) / np.float32(nd)).astype(
         np.float32
     )
-    table = np.concatenate([np.tile(np.cos(angles), 2), np.tile(np.sin(angles), 2)])
-    table = jnp.asarray(np.broadcast_to(table.astype(np.float32)[:, None], (2 * pair, width)))
-
-    first = lax.axis_index("freq") * band
-    lines = jnp.concatenate(
-        [
-            (quadruplet - (first - margin)).astype(f32),
-            nonlinear_coef[None],
-            wind_profile[None],
-            momentum * wind_profile[None],
-            jnp.zeros((2, nbins), f32),
-        ]
-    )
-    lines = lax.dynamic_slice_in_dim(jnp.pad(lines, ((0, 0), (margin, margin))), first, ext, 1)
-    cols = lines.T
+    waves = np.zeros((8, 128), np.float32)
+    waves[0, :pair], waves[1, :pair] = np.tile(np.cos(angles), 2), np.tile(np.sin(angles), 2)
 
     packed = -(-nf * half // 8) * 8
     peers = n_lat * n_freq - 1
     small = 8 + 2 * all_rows
+    share = (width // n_freq) * all_rows
+    span = -(-(nbins + margin) // 128) * 128
     vmem = pl.BlockSpec(memory_space=VMEM)
     sizes = (n_lat, n_lon, n_freq, nf, nd, rows, nbins)
     dma = pltpu.SemaphoreType.DMA
-    moved, energy, stress = pl.pallas_call(
+    out, ocean = pl.pallas_call(
         functools.partial(propagate_kernel, sizes),
         out_shape=(
-            jax.ShapeDtypeStruct((ext, rows * width), f32),
-            jax.ShapeDtypeStruct((8, width), f32),
-            jax.ShapeDtypeStruct((2 * all_rows, width), f32),
+            jax.ShapeDtypeStruct((band * rows, width), f32),
+            jax.ShapeDtypeStruct((2, share), f32),
         ),
         in_specs=[
             pl.BlockSpec(memory_space=pltpu.SMEM),
             pl.BlockSpec(memory_space=pl.ANY),
-            vmem, vmem, vmem, vmem, vmem,
-        ],
-        out_specs=(vmem, vmem, vmem),
+        ]
+        + [vmem] * 9,
+        out_specs=(pl.BlockSpec(memory_space=pl.ANY), vmem),
         scratch_shapes=[
             VMEM((band * rows, width), f32),
+            VMEM((ext, rows * width), f32),
+            VMEM((ext, rows * width), f32),
+            VMEM((band * rows, width), f32),
+            VMEM((2 * pair, width), f32),
+            VMEM((-(-ext // 128) * 128, 8), f32),
+            VMEM((8, span), f32),
             VMEM((packed, width), f32),
             VMEM((packed, width), f32),
             VMEM((packed, width), f32),
@@ -374,29 +429,27 @@
             VMEM((pair, width), f32),
             VMEM((small, width), f32),
             VMEM((peers, small, width), f32),
-            dma, dma((6,)), dma((6,)), dma((2,)), dma((2,)), dma((2,)), dma((2,)),
+            dma, dma((nf // 2,)),
+            dma((6,)), dma((6,)), dma((2,)), dma((2,)), dma((2,)), dma((2,)),
             dma((peers,)), dma((peers,)),
         ],
-        compiler_params=pltpu.CompilerParams(collective_id=0, has_side_effects=True),
+        compiler_params=pltpu.CompilerParams(
+            collective_id=0, has_side_effects=True, vmem_limit_bytes=24 << 20
+        ),
     )(
         group_speed,
         spectrum.reshape(band * rows, width),
-        table,
-        cols,
+        jnp.asarray(waves),
+        wind_profile,
+        nonlinear_coef,
+        momentum,
+        quadruplet,
         sea_mask,
         wind_growth,
+        dissipation,
         ocean_cell,
     )
-    out = pl.pallas_call(
-        functools.partial(source_kernel, nf, nd, rows),
-        out_shape=jax.ShapeDtypeStruct((band * rows, width), f32),
-        in_specs=[vmem] * 7,
-        out_specs=vmem,
-        scratch_shapes=[VMEM((ext, rows * width), f32)],
-    )(moved, cols, lines, sea_mask, wind_growth, dissipation, energy)
-    share = width // n_freq
-    ocean = stress[:, :share].reshape(2, all_rows, share).transpose(2, 1, 0)
-    return out.reshape(spectrum.shape), ocean.reshape(share * all_rows, 2)
+    return out.reshape(spectrum.shape), ocean.T
 
 
 def solution(mesh):

time: 35.2 us -> 35.6 us (1.011)
  local copies, waits for them, and re-layouts: 5.46 us -> 9.84 us
  Pallas kernels: 27.1 us -> 24.6 us
  other arithmetic: 1.43 us -> 0 us
    unnamed x2 -> x24, local copies, waits for them, and re-layouts: 0.01 us -> 9.84 us
    pallas_call x1 -> x0, Pallas kernels: 5.37 us -> none  [local(): pl.pallas_call(functools.partial(source_kernel, nf, nd, rows), out_shape=...]
    pallas_call x1, Pallas kernels: 21.7 us -> 24.6 us  [local(): pl.pallas_call(functools.partial(propagate_kernel, sizes), out_shape=(jax...]
    broadcast_in_dim x3 -> x0, local copies, waits for them, and re-layouts: 1.41 us -> none  [the longest x1 0.7 us: local(): nonlinear_coef[None]]
    another operation x1 -> x0, local copies, waits for them, and re-layouts: 1.4 us -> none
    transpose x2 -> x0, local copies, waits for them, and re-layouts: 1.11 us -> none  [local(): cols = lines.T]
    reshape x3 -> x0, local copies, waits for them, and re-layouts: 0.79 us -> none  [the longest x1 0.7 us: local(): return (out.reshape(spectrum.shape), ocean.reshape(share * all_rows, 2))]
    mul x1 -> x0, other arithmetic: 0.72 us -> none  [local(): momentum * wind_profile[None]]
where the time goes in v2:
time: 35.6 us; the launch traced here: 35.1 us
  Pallas kernels  24.6 us (69%)
  local copies, waits for them, and re-layouts  9.84 us (28%)
  between operations  0.66 us (2%)
    pallas_call x1, Pallas kernels, local(): pl.pallas_call(functools.partial(propagate_kernel, sizes), out_shape=(jax...  24.6 us
    unnamed x24, local copies, waits for them, and re-layouts  9.84 us

profile of v2, /device:TPU:0, one launch (start us, length us, event | category | flops | bytes accessed | tf_op | source)
XLA Modules:
  0.0 35.1 jit_solution(12497852598734212463)
XLA Ops:
  0.6 0.0 copy-start
  0.6 1.3 %copy-done = f32[18,36,4,128]{3,2,1,0:T(4,128)S(1)} copy-done((f32[18,36,4,128]{3,2,1,0:T(4,128)S(1)}, f32[18,36,4,128]{3,2,1,0:T(4,128)}, u32[]{:S(2)}) %copy-start) | copy-done | bytes 1327128
  2.0 0.0 copy-start.1
  2.0 0.7 %copy-done.1 = f32[2,1296]{1,0:T(2,128)S(1)} copy-done((f32[2,1296]{1,0:T(2,128)S(1)}, f32[2,1296]{1,0:T(2,128)}, u32[]{:S(2)}) %copy-start.1) | copy-done | bytes 10392
  2.7 0.0 copy-start.2
  2.7 0.7 %copy-done.2 = s32[2,1296]{1,0:T(2,128)S(1)} copy-done((s32[2,1296]{1,0:T(2,128)S(1)}, s32[2,1296]{1,0:T(2,128)}, u32[]{:S(2)}) %copy-start.2) | copy-done | bytes 10392
  3.4 0.0 copy-start.3
  3.4 0.7 %copy-done.3 = f32[1296]{0:T(1024)S(1)} copy-done((f32[1296]{0:T(1024)S(1)}, f32[1296]{0:T(1024)}, u32[]{:S(2)}) %copy-start.3) | copy-done | bytes 5208
  4.1 0.0 copy-start.4
  4.1 0.7 %copy-done.4 = f32[1296]{0:T(1024)S(1)} copy-done((f32[1296]{0:T(1024)S(1)}, f32[1296]{0:T(1024)}, u32[]{:S(2)}) %copy-start.4) | copy-done | bytes 5208
  4.8 0.0 copy-start.5
  4.8 0.7 %copy-done.5 = f32[8,128]{1,0:T(8,128)S(1)} copy-done((f32[8,128]{1,0:T(8,128)S(1)}, f32[8,128]{1,0:T(8,128)}, u32[]{:S(2)}) %copy-start.5) | copy-done | bytes 4120
  5.4 0.0 copy-start.6
  5.5 0.7 %copy-done.6 = s32[4,128]{1,0:T(4,128)S(1)} copy-done((s32[4,128]{1,0:T(4,128)S(1)}, s32[4,128]{1,0:T(4,128)}, u32[]{:S(2)}) %copy-start.6) | copy-done | bytes 2072
  6.1 0.0 copy-start.7
  6.1 0.7 %copy-done.7 = f32[4,128]{1,0:T(4,128)S(1)} copy-done((f32[4,128]{1,0:T(4,128)S(1)}, f32[4,128]{1,0:T(4,128)}, u32[]{:S(2)}) %copy-start.7) | copy-done | bytes 2072
  6.8 0.0 copy-start.8
  6.8 0.7 %copy-done.8 = f32[4,128]{1,0:T(4,128)S(1)} copy-done((f32[4,128]{1,0:T(4,128)S(1)}, f32[4,128]{1,0:T(4,128)}, u32[]{:S(2)}) %copy-start.8) | copy-done | bytes 2072
  7.5 0.0 copy-start.9
  7.5 0.7 %copy-done.9 = s32[4,128]{1,0:T(4,128)S(1)} copy-done((s32[4,128]{1,0:T(4,128)S(1)}, s32[4,128]{1,0:T(4,128)}, u32[]{:S(2)}) %copy-start.9) | copy-done | bytes 2072
  8.2 0.7 %copy-done.10 = f32[18]{0:T(128)S(1)} copy-done((f32[18]{0:T(128)S(1)}, f32[18]{0:T(128)}, u32[]{:S(2)}) %copy-start.10) | copy-done | bytes 96
  8.8 24.6 %shard_map.122 = (f32[2592,128]{1,0:T(8,128)S(1)}, f32[2,512]{1,0:T(2,128)S(1)}) custom-call(f32[18]{0:T(128)S(1)} %copy-done.10, f32[2592,128]{1,0:T(8,128)S(1)} %bitcast.3, f32[8,128]{1,0:T(8,128)S(1)} %copy-done.5, f32[1296]{0:T(1024)S(1)} %copy-done.3, f32[1296]{0:T(1024)S(1)} %copy-done.4, f32[2,1296]{1,0:T(2,128)S(1)} %copy-done.1, ...), custom_call_target="tpu_custom_call" | custom-call | tf_op jit(solution)/shard_map/pallas_call | solution.py:402
  33.4 1.1 %copy.15 = f32[18,36,4,128]{3,2,1,0:T(4,128)} copy(f32[18,36,4,128]{3,2,1,0:T(4,128)S(1)} %bitcast.4) | data formatting | bytes 2654208
  34.5 0.6 %copy.16 = f32[512,2]{0,1:T(2,128)} copy(f32[512,2]{0,1:T(2,128)S(1)} %bitcast.5) | data formatting | bytes 8192
  (1 shorter events, 0.0 us)
Async XLA Ops:
  0.6 1.3 %copy-start = (f32[18,36,4,128]{3,2,1,0:T(4,128)S(1)}, f32[18,36,4,128]{3,2,1,0:T(4,128)}, u32[]{:S(2)}) copy-start(f32[18,36,4,128]{3,2,1,0:T(4,128)} %param.11) | copy-start | bytes 3981316
  2.0 0.7 %copy-start.1 = (f32[2,1296]{1,0:T(2,128)S(1)}, f32[2,1296]{1,0:T(2,128)}, u32[]{:S(2)}) copy-start(f32[2,1296]{1,0:T(2,128)} %momentum.1) | copy-start | bytes 31108
  2.7 0.7 %copy-start.2 = (s32[2,1296]{1,0:T(2,128)S(1)}, s32[2,1296]{1,0:T(2,128)}, u32[]{:S(2)}) copy-start(s32[2,1296]{1,0:T(2,128)} %quad.1) | copy-start | bytes 31108
  3.4 0.7 %copy-start.3 = (f32[1296]{0:T(1024)S(1)}, f32[1296]{0:T(1024)}, u32[]{:S(2)}) copy-start(f32[1296]{0:T(1024)} %profile.1) | copy-start | bytes 15556
  4.1 0.7 %copy-start.4 = (f32[1296]{0:T(1024)S(1)}, f32[1296]{0:T(1024)}, u32[]{:S(2)}) copy-start(f32[1296]{0:T(1024)} %coef.1) | copy-start | bytes 15556
  4.8 0.7 %copy-start.5 = (f32[8,128]{1,0:T(8,128)S(1)}, f32[8,128]{1,0:T(8,128)}, u32[]{:S(2)}) copy-start(f32[8,128]{1,0:T(8,128)} %constant.2.clone.waves) | copy-start | bytes 12292
  5.4 0.7 %copy-start.6 = (s32[4,128]{1,0:T(4,128)S(1)}, s32[4,128]{1,0:T(4,128)}, u32[]{:S(2)}) copy-start(s32[4,128]{1,0:T(4,128)} %mask.1) | copy-start | bytes 6148
  6.1 0.7 %copy-start.7 = (f32[4,128]{1,0:T(4,128)S(1)}, f32[4,128]{1,0:T(4,128)}, u32[]{:S(2)}) copy-start(f32[4,128]{1,0:T(4,128)} %wind.1) | copy-start | bytes 6148
  6.8 0.7 %copy-start.8 = (f32[4,128]{1,0:T(4,128)S(1)}, f32[4,128]{1,0:T(4,128)}, u32[]{:S(2)}) copy-start(f32[4,128]{1,0:T(4,128)} %dissip.1) | copy-start | bytes 6148
  7.5 0.7 %copy-start.9 = (s32[4,128]{1,0:T(4,128)S(1)}, s32[4,128]{1,0:T(4,128)}, u32[]{:S(2)}) copy-start(s32[4,128]{1,0:T(4,128)} %cells.1) | copy-start | bytes 6148
  8.2 0.7 %copy-start.10 = (f32[18]{0:T(128)S(1)}, f32[18]{0:T(128)}, u32[]{:S(2)}) copy-start(f32[18]{0:T(128)} %speed.1) | copy-start | bytes 220

commit v3 on v2

--- a/solution.py
+++ b/solution.py
@@ -19,12 +19,18 @@
 
 
 def propagate_kernel(
-    sizes, speed, spectrum, waves, profile, coef, momentum, quad, mask, wind, dissip, cells,
-    out, stress,
-    x, moved, trans, result, table, cols, lines, pack_up, pack_down, got_up, got_down, edge_rows, lon_pack, got_left, got_right,
-    part, parts,
-    load_sem, store_sem, lat_send, lat_recv, lon_send, lon_recv, freq_send, freq_recv, part_send, part_recv,
+    sizes, spectrum, *refs
 ):
+    sources, refs = refs[:10], refs[10:]
+    out, stress, *refs = refs
+    inputs, refs = refs[:10], refs[10:]
+    speed, waves, profile, coef, momentum, quad, mask, wind, dissip, cells = inputs
+    (
+        x, moved, trans, result, table, rates, cols, lines, pack_up, pack_down, got_up, got_down,
+        edge_rows, lon_pack, got_left, got_right, part, parts,
+        load_sem, store_sem, small_sem, lat_send, lat_recv, lon_send, lon_recv, freq_send, freq_recv,
+        part_send, part_recv,
+    ) = refs
     n_lat, n_lon, n_freq, nf, nd, rows, nbins = sizes
     half = nd // 2
     pair = 2 * nd
@@ -34,6 +40,12 @@
     li, lo, fi = lax.axis_index("lat"), lax.axis_index("lon"), lax.axis_index("freq")
     load = pltpu.make_async_copy(spectrum, x, load_sem)
     load.start()
+    small = [
+        pltpu.make_async_copy(a, b, small_sem.at[i])
+        for i, (a, b) in enumerate(zip(sources, inputs))
+    ]
+    for copy in small:
+        copy.start()
 
     east, west = lax.rem(lo + 1, n_lon), lax.rem(lo + n_lon - 1, n_lon)
     group = []
@@ -88,7 +100,11 @@
     near = lax.div(n_freq - fi, n_freq)
     order = (near, 1 - near, 2)
 
+    for copy in small:
+        copy.wait()
     span = lines.shape[1]
+    rates[...] = jnp.zeros_like(rates)
+    rates[0:1, 0:nf] = speed[...].reshape(1, nf)
     lines[...] = jnp.zeros_like(lines)
     lines[0:2, 0:nbins] = (quad[...] - (fi * band - margin)).astype(jnp.float32)
     lines[2:3, 0:nbins] = coef[...].reshape(1, nbins)
@@ -177,8 +193,11 @@
             edge_rows[pl.ds(nd * f + half, half), :] = got_down[pl.ds(at, half), :]
 
     def chunk(c, sums):
+        rate = pltpu.roll(rates[...], 128 - 2 * c, 1)
         g = jnp.where(
-            lax.broadcasted_iota(jnp.int32, (pair, 128), 0) < nd, speed[2 * c], speed[2 * c + 1]
+            lax.broadcasted_iota(jnp.int32, (pair, 128), 0) < nd,
+            jnp.broadcast_to(rate[0:1, 0:1], (pair, 128)),
+            jnp.broadcast_to(rate[0:1, 1:2], (pair, 128)),
         )
         ax = g * jnp.abs(table[pl.ds(0, pair), :])
         ay = g * jnp.abs(table[pl.ds(pair, pair), :])
@@ -399,24 +418,34 @@
     vmem = pl.BlockSpec(memory_space=VMEM)
     sizes = (n_lat, n_lon, n_freq, nf, nd, rows, nbins)
     dma = pltpu.SemaphoreType.DMA
+    smalls = (
+        group_speed,
+        jnp.asarray(waves),
+        wind_profile,
+        nonlinear_coef,
+        momentum,
+        quadruplet,
+        sea_mask,
+        wind_growth,
+        dissipation,
+        ocean_cell,
+    )
     out, ocean = pl.pallas_call(
         functools.partial(propagate_kernel, sizes),
         out_shape=(
             jax.ShapeDtypeStruct((band * rows, width), f32),
             jax.ShapeDtypeStruct((2, share), f32),
         ),
-        in_specs=[
-            pl.BlockSpec(memory_space=pltpu.SMEM),
-            pl.BlockSpec(memory_space=pl.ANY),
-        ]
-        + [vmem] * 9,
-        out_specs=(pl.BlockSpec(memory_space=pl.ANY), vmem),
-        scratch_shapes=[
+        in_specs=[pl.BlockSpec(memory_space=pltpu.HBM)] * 11,
+        out_specs=(pl.BlockSpec(memory_space=pltpu.HBM), vmem),
+        scratch_shapes=[VMEM(a.shape, a.dtype) for a in smalls]
+        + [
             VMEM((band * rows, width), f32),
             VMEM((ext, rows * width), f32),
             VMEM((ext, rows * width), f32),
             VMEM((band * rows, width), f32),
             VMEM((2 * pair, width), f32),
+            VMEM((8, width), f32),
             VMEM((-(-ext // 128) * 128, 8), f32),
             VMEM((8, span), f32),
             VMEM((packed, width), f32),
@@ -429,26 +458,14 @@
             VMEM((pair, width), f32),
             VMEM((small, width), f32),
             VMEM((peers, small, width), f32),
-            dma, dma((nf // 2,)),
+            dma, dma((nf // 2,)), dma((len(smalls),)),
             dma((6,)), dma((6,)), dma((2,)), dma((2,)), dma((2,)), dma((2,)),
             dma((peers,)), dma((peers,)),
         ],
         compiler_params=pltpu.CompilerParams(
-            collective_id=0, has_side_effects=True, vmem_limit_bytes=24 << 20
+            collective_id=0, has_side_effects=True
         ),
-    )(
-        group_speed,
-        spectrum.reshape(band * rows, width),
-        jnp.asarray(waves),
-        wind_profile,
-        nonlinear_coef,
-        momentum,
-        quadruplet,
-        sea_mask,
-        wind_growth,
-        dissipation,
-        ocean_cell,
-    )
+    )(spectrum.reshape(band * rows, width), *smalls)
     return out.reshape(spectrum.shape), ocean.T
 
 

time: 35.6 us -> 28.6 us (0.80); the launches traced: 35.1 us -> 28.5 us
  local copies, waits for them, and re-layouts: 9.84 us -> 3.07 us
    unnamed x24 -> x4, local copies, waits for them, and re-layouts: 9.84 us -> 3.07 us
where the time goes in v3:
time: 28.6 us; the launch traced here: 28.5 us
  Pallas kernels  24.8 us (87%)
  local copies, waits for them, and re-layouts  3.07 us (11%)
  between operations  0.65 us (2%)
    pallas_call x1, Pallas kernels, local(): pl.pallas_call(functools.partial(propagate_kernel, sizes), out_shape=(jax...  24.8 us
    unnamed x4, local copies, waits for them, and re-layouts  3.07 us

profile of v3, /device:TPU:0, one launch (start us, length us, event | category | flops | bytes accessed | tf_op | source)
XLA Modules:
  0.0 28.5 jit_solution(14461453169788693316)
XLA Ops:
  0.6 24.8 %shard_map.122 = (f32[2592,128]{1,0:T(8,128)}, f32[2,512]{1,0:T(2,128)}) custom-call(f32[2592,128]{1,0:T(8,128)} %bitcast.3, f32[18]{0:T(128)} %refs_0_.1, f32[8,128]{1,0:T(8,128)} %constant.2.clone.refs_1_, f32[1296]{0:T(1024)} %refs_2_.1, f32[1296]{0:T(1024)} %refs_3_.1, f32[2,1296]{1,0:T(2,128)} %refs_4_.1, s32[2,1296]{1,0:T(2,128)} %refs_5_.1, ...), custom_call_target="tpu_custom_call" | custom-call | tf_op jit(solution)/shard_map/pallas_call | solution.py:433
  25.4 0.0 copy-start
  25.4 2.5 %copy.15 = f32[18,36,4,128]{3,2,1,0:T(4,128)} copy(f32[18,36,4,128]{3,2,1,0:T(4,128)} %bitcast.4) | data formatting | bytes 2654208
  27.9 0.0 copy-done
  27.9 0.6 %copy.16 = f32[512,2]{0,1:T(2,128)} copy(f32[512,2]{0,1:T(2,128)S(1)} %bitcast.5) | data formatting | bytes 8192
Async XLA Ops:
  25.4 2.5 %copy-start = (f32[2,512]{1,0:T(2,128)S(1)}, f32[2,512]{1,0:T(2,128)}, u32[]{:S(2)}) copy-start(f32[2,512]{1,0:T(2,128)} %get-tuple-element.5) | copy-start | bytes 12292

commit v4 on v3

--- a/solution.py
+++ b/solution.py
@@ -22,13 +22,13 @@
     sizes, spectrum, *refs
 ):
     sources, refs = refs[:10], refs[10:]
-    out, stress, *refs = refs
+    result, stress, *refs = refs
     inputs, refs = refs[:10], refs[10:]
     speed, waves, profile, coef, momentum, quad, mask, wind, dissip, cells = inputs
     (
-        x, moved, trans, result, table, rates, cols, lines, pack_up, pack_down, got_up, got_down,
+        x, moved, trans, table, rates, cols, lines, pack_up, pack_down, got_up, got_down,
         edge_rows, lon_pack, got_left, got_right, part, parts,
-        load_sem, store_sem, small_sem, lat_send, lat_recv, lon_send, lon_recv, freq_send, freq_recv,
+        load_sem, small_sem, lat_send, lat_recv, lon_send, lon_recv, freq_send, freq_recv,
         part_send, part_recv,
     ) = refs
     n_lat, n_lon, n_freq, nf, nd, rows, nbins = sizes
@@ -132,6 +132,7 @@
     low = row < half
     forward = table[pl.ds(0, pair), :] > 0.0
     rim = lane == jnp.where(forward, 0, 127)
+    sent = lane == jnp.where(forward, 127, 0)
 
     def shifted(e):
         return jnp.where(forward, pltpu.roll(e, 1, 1), pltpu.roll(e, 127, 1))
@@ -141,7 +142,7 @@
 
     def pack_step(c, acc):
         for r in range(rows):
-            z = jnp.where(rim, shifted(load_row(c, r)), 0.0)
+            z = jnp.where(sent, load_row(c, r), 0.0)
             acc = acc + pltpu.roll(z, c * rows + r, 1)
         return acc
 
@@ -201,7 +202,7 @@
         )
         ax = g * jnp.abs(table[pl.ds(0, pair), :])
         ay = g * jnp.abs(table[pl.ds(pair, pair), :])
-        halo = jnp.where(forward, got_left[...], got_right[...])
+        halo = got_left[...]
         at = pl.multiple_of(pair * c, 8)
         outer = edge_rows[pl.ds(at, pair), :]
         here = pl.multiple_of(margin + pair * c, 8)
@@ -227,6 +228,9 @@
     sums = tuple(jnp.zeros((8, 128), jnp.float32) for _ in range(3 * rows))
     lon_copy(True).wait_recv()
     lon_copy(False).wait_recv()
+    got_left[...] = jnp.where(
+        forward, pltpu.roll(got_left[...], 1, 1), pltpu.roll(got_right[...], 127, 1)
+    )
     for k in (near, 1 - near):
         receive(k, k * (nf - 4), 4)
         sums = lax.fori_loop(k * (nf // 2 - 2), k * (nf // 2 - 2) + 2, chunk, sums)
@@ -283,10 +287,6 @@
         )
         return carry
 
-    def store_copy(c):
-        here = pl.ds(pl.multiple_of(rows * pair * (c - 2), 8), rows * pair)
-        return pltpu.make_async_copy(result.at[here], out.at[here], store_sem.at[c - 2])
-
     def finish(c, carry):
         at = pl.multiple_of(pair * c, 8)
         prior = pl.multiple_of(pair * c - pair, 8)
@@ -306,7 +306,6 @@
             result[pl.ds(rows * pair * (c - 2) + r, pair, stride=rows), :] = mask[
                 r : r + 1, :
             ].astype(jnp.float32) * (e + time_step * tendency)
-        store_copy(c).start()
         return carry
 
     lax.fori_loop(t_from, t_to, interact, 0)
@@ -367,10 +366,6 @@
     @pl.when(fi < n_freq - 1)
     def _():
         freq_copy(True).wait_send()
-
-    for c in range(2, chunks - 2):
-        store_copy(c).wait()
-
 
 def split(v):
     high = v.astype(jnp.bfloat16)
@@ -437,13 +432,12 @@
             jax.ShapeDtypeStruct((2, share), f32),
         ),
         in_specs=[pl.BlockSpec(memory_space=pltpu.HBM)] * 11,
-        out_specs=(pl.BlockSpec(memory_space=pltpu.HBM), vmem),
+        out_specs=(vmem, vmem),
         scratch_shapes=[VMEM(a.shape, a.dtype) for a in smalls]
         + [
             VMEM((band * rows, width), f32),
             VMEM((ext, rows * width), f32),
             VMEM((ext, rows * width), f32),
-            VMEM((band * rows, width), f32),
             VMEM((2 * pair, width), f32),
             VMEM((8, width), f32),
             VMEM((-(-ext // 128) * 128, 8), f32),
@@ -458,14 +452,19 @@
             VMEM((pair, width), f32),
             VMEM((small, width), f32),
             VMEM((peers, small, width), f32),
-            dma, dma((nf // 2,)), dma((len(smalls),)),
+            dma, dma((len(smalls),)),
             dma((6,)), dma((6,)), dma((2,)), dma((2,)), dma((2,)), dma((2,)),
             dma((peers,)), dma((peers,)),
         ],
         compiler_params=pltpu.CompilerParams(
-            collective_id=0, has_side_effects=True
+            collective_id=0, has_side_effects=True, vmem_limit_bytes=24 << 20
         ),
-    )(spectrum.reshape(band * rows, width), *smalls)
+    )(
+        *[
+            pltpu.with_memory_space_constraint(a, pltpu.HBM)
+            for a in (spectrum.reshape(band * rows, width), *smalls)
+        ]
+    )
     return out.reshape(spectrum.shape), ocean.T
 
 

time: 28.6 us -> 24.8 us (0.87)
  Pallas kernels: 24.8 us -> 22.3 us
  local copies, waits for them, and re-layouts: 3.07 us -> 1.66 us
    pallas_call x1, Pallas kernels: 24.8 us -> 22.3 us  [local(): pl.pallas_call(functools.partial(propagate_kernel, sizes), out_shape=(jax...]
    unnamed x4 -> x2, local copies, waits for them, and re-layouts: 3.07 us -> 1.66 us
where the time goes in v4:
time: 24.8 us; the launch traced here: 24.6 us
  Pallas kernels  22.3 us (90%)
  local copies, waits for them, and re-layouts  1.66 us (7%)
  between operations  0.64 us (3%)
    pallas_call x1, Pallas kernels, local(): pl.pallas_call(functools.partial(propagate_kernel, sizes), out_shape=(jax...  22.3 us
    unnamed x2, local copies, waits for them, and re-layouts  1.66 us

profile of v4, /device:TPU:0, one launch (start us, length us, event | category | flops | bytes accessed | tf_op | source)
XLA Modules:
  0.0 24.6 jit_solution(4959642841825039462)
XLA Ops:
  0.6 22.3 %shard_map.122 = (f32[2592,128]{1,0:T(8,128)S(1)}, f32[2,512]{1,0:T(2,128)S(1)}) custom-call(f32[2592,128]{1,0:T(8,128)} %bitcast.5, f32[18]{0:T(128)} %refs_0_.1, f32[8,128]{1,0:T(8,128)} %constant.2.clone.refs_1_, f32[1296]{0:T(1024)} %refs_2_.1, f32[1296]{0:T(1024)} %refs_3_.1, f32[2,1296]{1,0:T(2,128)} %refs_4_.1, s32[2,1296]{1,0:T(2,128)} %refs_5_.1, ...), custom_call_target="tpu_custom_call" | custom-call | tf_op jit(solution)/shard_map/pallas_call | solution.py:428
  23.0 1.1 %copy.15 = f32[18,36,4,128]{3,2,1,0:T(4,128)} copy(f32[18,36,4,128]{3,2,1,0:T(4,128)S(1)} %bitcast.3) | data formatting | bytes 2654208
  24.0 0.6 %copy.16 = f32[512,2]{0,1:T(2,128)} copy(f32[512,2]{0,1:T(2,128)S(1)} %bitcast.4) | data formatting | bytes 8192
